TPU v7x, 32 devices: a whole 2x2x4 slice. The times are simulated.
32 devices in a mesh: band: 8 (over z, core), lane: 4 (over y, x).
Axes of the slice: x: 2, y: 2, z: 4, core: 2. Of those that a mesh axis runs over, the one named last changes fastest.
Arguments:
- first_factor: bfloat16 [8192, 4096], P('band', 'lane'), may hold values from -6 to 6
- second_factor: bfloat16 [4096, 2048], P('band', 'lane'), may hold values from -0.09375 to 0.09375
- result_in: float32 [8192, 2048], P('band', 'lane'), may hold values from -6 to 6
- pivot_scale: float32 [4096], replicated, may hold values from 0.25 to 1.75
Outputs:
- updated: float32 [8192, 2048], P('band', 'lane')
All inputs are finite; a program needn't handle non-finite values.
Results may differ from a plain program's by a relative error of at most 0.002.
Values may be sent and summed in bfloat16 or wider, within the bound.
A program may use at most 128 MiB of HBM per device.

v0:
```python
import jax
import jax.numpy as jnp
from jax import lax
from jax.sharding import PartitionSpec as P


def join_panel(left_panel, right_panel):
    return jnp.dot(left_panel, right_panel, preferred_element_type=jnp.float32)


def on_device(first_factor, second_factor, result_in, pivot_scale):
    share = first_factor.shape[1]
    part_scale = lax.dynamic_slice_in_dim(pivot_scale, lax.axis_index("lane") * share, share)
    scaled_left = (first_factor.astype(jnp.float32) * part_scale).astype(jnp.bfloat16)
    left_line = lax.all_gather(scaled_left, "lane", axis=1, tiled=True)
    total = join_panel(left_line, lax.all_gather(second_factor, "band", axis=0, tiled=True))
    updated = result_in - total
    row_power = lax.psum(jnp.sum(updated * updated, axis=1), "lane")
    updated = (
        updated * lax.rsqrt(row_power / (updated.shape[1] * lax.axis_size("lane")) + 1e-06)[:, None]
    )
    return updated


def solution(mesh):
    return jax.shard_map(
        on_device,
        mesh=mesh,
        in_specs=(P("band", "lane"), P("band", "lane"), P("band", "lane"), P()),
        out_specs=P("band", "lane"),
        check_vma=False,
    )
```

profile of v0, /device:TPU:0, one launch (start us, length us, event | category | flops | bytes accessed | tf_op | source)
XLA Modules:
  0.0 177.2 jit_solution(5245780658395474004)
XLA Ops:
  6.5 0.0 all-gather.5.cloned.1.call-start
  6.5 0.7 all-gather.5.cloned.1.call-update
  7.3 0.0 all-gather.3.cloned.1.call-start
  7.3 0.7 dynamic_slice.3
  8.0 3.5 %multiply_convert_fusion = bf16[1024,1024]{1,0:T(8,128)(2,1)} fusion(bf16[1024,1024]{1,0:T(8,128)(2,1)} %param.4, f32[1024]{0:T(1024)S(1)} %dynamic_slice.3), kind=kLoop, calls=%fused_computation | loop fusion | flops 3145728 | bytes 4198400 | tf_op jit(solution)/shard_map/convert_element_type | solution.py:14
  11.5 0.0 copy-start
  11.5 0.0 all-gather.3.cloned.1.call-update
  11.5 1.6 copy-done
  13.1 1.8 %copy.5 = f32[1024,512]{0,1:T(8,128)} copy(f32[1024,512]{1,0:T(8,128)S(1)} %copy-done) | data formatting | bytes 4194304 | tf_op args[2]
  14.9 43.7 %all-gather.5.cloned.1.call-done = bf16[4096,512]{1,0:T(8,128)(2,1)} async-done(((bf16[512,512]{1,0:T(8,128)(2,1)}), bf16[4096,512]{1,0:T(8,128)(2,1)}) %all-gather.5.cloned.1.call-update) | async-done | bytes 4194320 | tf_op jit(solution)/shard_map/all_gather | solution.py:16
  58.6 88.2 %all-gather.3.cloned.1.call-done = bf16[1024,4096]{1,0:T(8,128)(2,1)} async-done(((bf16[1024,1024]{1,0:T(8,128)(2,1)}), bf16[1024,4096]{1,0:T(8,128)(2,1)}) %all-gather.3.cloned.1.call-update) | async-done | bytes 8388624 | tf_op jit(solution)/shard_map/all_gather | solution.py:15
  146.7 11.1 %multiply_reduce_fusion = (f32[1024]{0:T(1024)S(1)}, f32[1024,512]{0,1:T(8,128)}) fusion(f32[1024,512]{0,1:T(8,128)} %copy.5, bf16[1024,4096]{1,0:T(8,128)(2,1)} %all-gather.3.cloned.1.call-done, bf16[4096,512]{1,0:T(8,128)(2,1)} %all-gather.5.cloned.1.call-done), kind=kOutput, calls=%fused_computation.1 | convolution fusion | flops 4296539136 | bytes 16781312 | tf_op jit(solution)/shard_map/dot_general | solution.py:8
  157.8 8.9 %psum.7 = f32[1024]{0:T(1024)S(1)} all-reduce(f32[1024]{0:T(1024)S(1)} %get-tuple-element.5), channel_id=1, replica_groups=mesh['band'=8,'lane'=4] {'lane'}, use_global_device_ids=true, to_apply=%region_1.0 | all-reduce | flops 1024 | bytes 8192 | tf_op jit(solution)/shard_map/psum | solution.py:18
  166.7 1.8 %broadcast_multiply_fusion = f32[1024,512]{0,1:T(8,128)S(1)} fusion(f32[1024,512]{0,1:T(8,128)} %get-tuple-element.6, f32[1024]{0:T(1024)S(1)} %add_rsqrt_fusion), kind=kLoop, calls=%fused_computation.3 | loop fusion | flops 524288 | bytes 4198400 | tf_op jit(solution)/shard_map/mul | solution.py:20
  168.6 1.8 %copy.6 = f32[1024,512]{1,0:T(8,128)} copy(f32[1024,512]{0,1:T(8,128)S(1)} %broadcast_multiply_fusion) | data formatting | bytes 4194304 | tf_op jit(solution)/shard_map/mul | solution.py:20
  (1 shorter events, 0.0 us)
Async XLA Ops:
  6.5 52.0 %all-gather.5.cloned.1.call-start = ((), (), s32[]{:S(2)}) async-start(), calls=%async_computation.1 | async-start | bytes 4718592 | tf_op jit(solution)/shard_map/all_gather | solution.py:16
  7.3 139.5 %all-gather.3.cloned.1.call-start = ((), (), s32[]{:S(2)}) async-start(), calls=%async_computation | async-start | bytes 10485760 | tf_op jit(solution)/shard_map/all_gather | solution.py:15
  11.5 1.6 copy-start
Sparse Core Ops, SparseCore 0:
  8.9 49.5 all-gather.4
  60.4 86.2 all-gather.2
where the time goes:
time: 177 us
  waiting for transfers between devices  133 us (75%)
  between operations  13.4 us (8%)
  matrix products  11.1 us (6%)
  blocking collectives  8.9 us (5%)
  local copies, waits for them, and re-layouts  5.88 us (3%)
  other arithmetic  5.32 us (3%)
    all_gather x1, waiting for transfers between devices, on_device(): left_line = lax.all_gather(scaled_left, 'lane', axis=1, tiled=True)  88.2 us
    all_gather x1, waiting for transfers between devices, on_device(): lax.all_gather(second_factor, 'band', axis=0, tiled=True)  43.7 us
    dot_general x1, matrix products, join_panel(): return jnp.dot(left_panel, right_panel, preferred_element_type=jnp.float32)  11.1 us
    psum x1, blocking collectives, on_device(): row_power = lax.psum(jnp.sum(updated * updated, axis=1), 'lane')  8.9 us
  transfers between devices with their start and end apart: 2, of which 2 were waited for; matrix products, arithmetic and copies ran while one was open for 3% of the time, Pallas kernels for 0%

commit v1 on v0

--- a/solution.py
+++ b/solution.py
@@ -2,6 +2,14 @@
 import jax.numpy as jnp
 from jax import lax
 from jax.sharding import PartitionSpec as P
+
+
+def gather_from_all(array, axis, dim):
+    size = lax.axis_size(axis)
+    repeats = [size if d == dim else 1 for d in range(array.ndim)]
+    return lax.all_to_all(
+        jnp.tile(array, repeats), axis, split_axis=dim, concat_axis=dim, tiled=True
+    )
 
 
 def join_panel(left_panel, right_panel):
@@ -13,7 +21,7 @@
     part_scale = lax.dynamic_slice_in_dim(pivot_scale, lax.axis_index("lane") * share, share)
     scaled_left = (first_factor.astype(jnp.float32) * part_scale).astype(jnp.bfloat16)
     left_line = lax.all_gather(scaled_left, "lane", axis=1, tiled=True)
-    total = join_panel(left_line, lax.all_gather(second_factor, "band", axis=0, tiled=True))
+    total = join_panel(left_line, gather_from_all(second_factor, "band", 0))
     updated = result_in - total
     row_power = lax.psum(jnp.sum(updated * updated, axis=1), "lane")
     updated = (

time: 177 us -> 146 us (0.82)
  waiting for transfers between devices: 133 us -> 92.3 us
  starting transfers between devices: 0.04 us -> 6.49 us
    all_to_all x0 -> x1, waiting for transfers between devices: none -> 92.3 us  [gather_from_all(): lax.all_to_all(jnp.tile(array, repeats), axis, split_axis=dim, concat_axi...]
    all_gather x1, waiting for transfers between devices: 88.2 us -> 0.01 us  [on_device(): left_line = lax.all_gather(scaled_left, 'lane', axis=1, tiled=True)]
    all_gather x1 -> x0, waiting for transfers between devices: 43.7 us -> none  [on_device(): lax.all_gather(second_factor, 'band', axis=0, tiled=True)]
    all_to_all x0 -> x1, starting transfers between devices: none -> 6.49 us  [gather_from_all(): lax.all_to_all(jnp.tile(array, repeats), axis, split_axis=dim, concat_axi...]
    another operation x0 -> x1, local copies, waits for them, and re-layouts: none -> 2.3 us  [gather_from_all(): jnp.tile(array, repeats)]
  transfers between devices with their start and end apart: 2 -> 2, of which waited for: 2 -> 1; matrix products, arithmetic and copies ran while one was open for 3% -> 3% of each run, Pallas kernels for 0% -> 0%
where the time goes in v1:
time: 146 us
  waiting for transfers between devices  92.3 us (63%)
  between operations  13.4 us (9%)
  matrix products  11.1 us (8%)
  blocking collectives  9.88 us (7%)
  local copies, waits for them, and re-layouts  7.64 us (5%)
  starting transfers between devices  6.49 us (4%)
  other arithmetic  5.32 us (4%)
    all_to_all x1, waiting for transfers between devices, gather_from_all(): lax.all_to_all(jnp.tile(array, repeats), axis, split_axis=dim, concat_axi...  92.3 us
    dot_general x1, matrix products, join_panel(): return jnp.dot(left_panel, right_panel, preferred_element_type=jnp.float32)  11.1 us
    psum x1, blocking collectives, on_device(): row_power = lax.psum(jnp.sum(updated * updated, axis=1), 'lane')  9.88 us
    all_to_all x1, starting transfers between devices, gather_from_all(): lax.all_to_all(jnp.tile(array, repeats), axis, split_axis=dim, concat_axi...  6.49 us
    convert_element_type x1, other arithmetic, on_device(): (first_factor.astype(jnp.float32) * part_scale).astype(jnp.bfloat16)  3.5 us
  transfers between devices with their start and end apart: 2, of which 1 were waited for; matrix products, arithmetic and copies ran while one was open for 3% of the time, Pallas kernels for 0%

profile of v1, /device:TPU:0, one launch (start us, length us, event | category | flops | bytes accessed | tf_op | source)
XLA Modules:
  0.0 146.1 jit_solution(2642336143959886845)
XLA Ops:
  6.5 0.0 all-gather.2.cloned.1.call-start
  6.5 0.7 dynamic_slice.3
  7.2 3.5 %multiply_convert_fusion = bf16[1024,1024]{1,0:T(8,128)(2,1)} fusion(bf16[1024,1024]{1,0:T(8,128)(2,1)} %param.4, f32[1024]{0:T(1024)S(1)} %dynamic_slice.3), kind=kLoop, calls=%fused_computation | loop fusion | flops 3145728 | bytes 4198400 | tf_op jit(solution)/shard_map/convert_element_type | solution.py:22
  10.7 0.0 copy-start.1
  10.7 0.0 all-gather.2.cloned.1.call-update
  10.7 1.0 copy-done.1
  11.8 2.3 %tile.2 = bf16[8,512,512]{2,1,0:T(8,128)(2,1)} broadcast(bf16[512,512]{1,0:T(8,128)(2,1)S(1)} %copy-done.1), dimensions={1,2} | broadcast | bytes 4718592 | tf_op jit(solution)/shard_map/tile | solution.py:11
  14.1 0.0 copy-start
  14.1 6.5 %all-to-all-start = ((bf16[8,512,512]{2,1,0:T(8,128)(2,1)}), bf16[8,512,512]{2,1,0:T(8,128)(2,1)}, u32[]{:S(2)}, u32[]{:S(2)}) async-start(bf16[8,512,512]{2,1,0:T(8,128)(2,1)} %tile.2), calls=%async_computation | async-start | bytes 8388608 | tf_op jit(solution)/shard_map/all_to_all | solution.py:10
  20.6 0.0 copy-done
  20.6 1.8 %copy.5 = f32[1024,512]{0,1:T(8,128)} copy(f32[1024,512]{1,0:T(8,128)S(1)} %copy-done) | data formatting | bytes 4194304 | tf_op args[2]
  22.4 92.3 %all-to-all-done = bf16[8,512,512]{2,1,0:T(8,128)(2,1)} async-done(((bf16[8,512,512]{2,1,0:T(8,128)(2,1)}), bf16[8,512,512]{2,1,0:T(8,128)(2,1)}, u32[]{:S(2)}, u32[]{:S(2)}) %all-to-all-start) | async-done | bytes 4194336 | tf_op jit(solution)/shard_map/all_to_all | solution.py:10
  114.6 0.0 all-gather.2.cloned.1.call-done
  114.6 11.1 %multiply_reduce_fusion = (f32[1024]{0:T(1024)S(1)}, f32[1024,512]{0,1:T(8,128)}) fusion(f32[1024,512]{0,1:T(8,128)} %copy.5, bf16[1024,4096]{1,0:T(8,128)(2,1)} %all-gather.2.cloned.1.call-done, bf16[4096,512]{1,0:T(8,128)(2,1)} %bitcast), kind=kOutput, calls=%fused_computation.1 | convolution fusion | flops 4296539136 | bytes 16781312 | tf_op jit(solution)/shard_map/dot_general | solution.py:16
  125.8 9.9 %psum.7 = f32[1024]{0:T(1024)S(1)} all-reduce(f32[1024]{0:T(1024)S(1)} %get-tuple-element.5), channel_id=1, replica_groups=mesh['band'=8,'lane'=4] {'lane'}, use_global_device_ids=true, to_apply=%region_1.0 | all-reduce | flops 1024 | bytes 8192 | tf_op jit(solution)/shard_map/psum | solution.py:26
  135.6 1.8 %broadcast_multiply_fusion = f32[1024,512]{0,1:T(8,128)S(1)} fusion(f32[1024,512]{0,1:T(8,128)} %get-tuple-element.6, f32[1024]{0:T(1024)S(1)} %add_rsqrt_fusion), kind=kLoop, calls=%fused_computation.3 | loop fusion | flops 524288 | bytes 4198400 | tf_op jit(solution)/shard_map/mul | solution.py:28
  137.5 1.8 %copy.6 = f32[1024,512]{1,0:T(8,128)} copy(f32[1024,512]{0,1:T(8,128)S(1)} %broadcast_multiply_fusion) | data formatting | bytes 4194304 | tf_op jit(solution)/shard_map/mul | solution.py:28
  (1 shorter events, 0.0 us)
Async XLA Ops:
  6.5 108.1 %all-gather.2.cloned.1.call-start = ((), (), s32[]{:S(2)}) async-start(), calls=%async_computation.1 | async-start | bytes 10485760 | tf_op jit(solution)/shard_map/all_gather | solution.py:23
  10.7 1.0 copy-start.1
  14.1 6.5 %copy-start = (f32[1024,512]{1,0:T(8,128)S(1)}, f32[1024,512]{1,0:T(8,128)}, u32[]{:S(2)}) copy-start(f32[1024,512]{1,0:T(8,128)} %param.6) | copy-start | bytes 6291460
  14.1 100.6 %all-to-all-start = ((bf16[8,512,512]{2,1,0:T(8,128)(2,1)}), bf16[8,512,512]{2,1,0:T(8,128)(2,1)}, u32[]{:S(2)}, u32[]{:S(2)}) async-start(bf16[8,512,512]{2,1,0:T(8,128)(2,1)} %tile.2), calls=%async_computation | async-start | bytes 8388608 | tf_op jit(solution)/shard_map/all_to_all | solution.py:10
Sparse Core Ops, SparseCore 0:
  10.9 90.1 all-gather.1
